TPU v7x, 256 devices: a whole 4x4x8 slice. The times are simulated.
256 devices in a mesh: dp: 8 (over y, core), expert: 8 (over z), tile: 4 (over x).
Axes of the slice: x: 4, y: 4, z: 8, core: 2. Of those that a mesh axis runs over, the one named last changes fastest.
Arguments:
- tokens: bfloat16 [4096, 4096], P(('dp', 'expert'), 'tile'), may hold values from -6 to 6
- hidden: bfloat16 [4096, 2, 7168], P(('dp', 'expert'), None, 'tile'), may hold values from -6 to 6
- routes: int32 [4096, 2], P(('dp', 'expert')), may hold values from 0 to 7, all different within a row; in each aligned block of 64 rows (0 to 63, 64 to 127, ...) at most 24 rows name the same one
- lengths: int32 [64], P(('dp', 'expert')), may hold values from 1 to 64, as said below
Outputs:
- hessian_in: float32 [8, 4096, 4096], P('expert', 'tile', 'dp')
- hessian_down: float32 [8, 7168, 7168], P('expert', 'tile', 'dp')
Inputs may be any that keep to these rules, and one draw needn't show every extreme that they name: `routes`: in each aligned block of 64 rows (the rows of one group) no expert is named by more than 24 rows, a bound that some block reaches. The live rows of group g are its first lengths[g] rows; the last group is full.
All inputs are finite; a program needn't handle non-finite values.
Results may differ from a plain program's by a relative error of at most 0.0003.
Values may be sent and summed in bfloat16 or wider, within the bound.
A program may use at most 64 MiB of HBM per device.

v0:
```python
import jax
import jax.numpy as jnp
from jax import lax
from jax.sharding import PartitionSpec as P


def sent_together(arrays, axis, split_dim, concat_dim, along):
    widths = [a.shape[along] for a in arrays]
    both = jnp.concatenate(arrays, axis=along)
    out = lax.all_to_all(both, axis, split_axis=split_dim, concat_axis=concat_dim, tiled=True)
    return tuple(jnp.split(out, [sum(widths[:k]) for k in range(1, len(widths))], axis=along))


def from_everyone(value, axis):
    copies = jnp.broadcast_to(value, (lax.axis_size(axis), *value.shape))
    return lax.all_to_all(copies, axis, split_axis=0, concat_axis=0, tiled=True)


def of_everyone(value, axis):
    everything = from_everyone(value, axis)
    return jnp.sum(everything, axis=0)


def side_by_side(arrays, axis, dim, along):
    ends, at = ([], 0)
    for a in arrays[:-1]:
        at += a.shape[along]
        ends.append(at)
    both = jnp.concatenate(arrays, axis=along)
    return tuple(jnp.split(lax.all_gather(both, axis, axis=dim, tiled=True), ends, axis=along))


def contract(left, right):
    return lax.dot_general(
        left, right, (((0,), (0,)), ((), ())), preferred_element_type=jnp.float32
    )


def dispatch_tables(routes, live_count, experts, share_size, senders):
    token_count = routes.shape[0]
    top_count = routes.shape[1]
    flat_routes = routes.reshape(token_count * top_count)
    pair_index = jnp.arange(token_count * top_count, dtype=jnp.int32)
    pair_live = pair_index // top_count < live_count
    expert_ids = jnp.arange(experts, dtype=jnp.int32)
    onehot = ((flat_routes[:, None] == expert_ids[None, :]) & pair_live[:, None]).astype(
        jnp.float32
    )
    before = jnp.cumsum(onehot, axis=0) - onehot
    position = jnp.sum(before * onehot, axis=1).astype(jnp.int32)
    target = (
        position // share_size * (experts * share_size)
        + flat_routes * share_size
        + position % share_size
    )
    slot_total = senders * experts * share_size
    placed = (target[None, :] == jnp.arange(slot_total, dtype=jnp.int32)[:, None]) & pair_live[
        None, :
    ]
    return (placed.astype(jnp.float32), jnp.sum(onehot, axis=0))


def on_device(tokens, hidden, routes, lengths):
    experts = lax.axis_size("expert")
    senders = lax.axis_size("dp")
    token_count = tokens.shape[0]
    top_count = routes.shape[1]
    share_size = (5 * token_count + 2 * experts * senders - 1) // (2 * experts * senders)
    placed, local_counts = dispatch_tables(routes, lengths[0], experts, share_size, senders)
    slot_total = placed.shape[0]
    by_token = jnp.sum(placed.reshape(slot_total, token_count, top_count), axis=2).astype(
        jnp.bfloat16
    )
    send_tokens = jnp.dot(by_token, tokens, preferred_element_type=jnp.float32).astype(jnp.bfloat16)
    flat_hidden = hidden.reshape(token_count * top_count, hidden.shape[2])
    send_hidden = jnp.dot(
        placed.astype(jnp.bfloat16), flat_hidden, preferred_element_type=jnp.float32
    ).astype(jnp.bfloat16)
    slot_tokens, slot_hidden = sent_together((send_tokens, send_hidden), ("dp", "expert"), 0, 0, 1)
    global_counts = of_everyone(local_counts, ("dp", "expert"))
    own_expert = lax.axis_index("expert")
    own_count = jnp.sum(
        jnp.where(jnp.arange(experts, dtype=jnp.int32) == own_expert, global_counts, 0.0)
    )
    factor = 2.0 / jnp.maximum(own_count, 1.0)
    full_tokens, full_hidden = (
        lax.all_gather(slot_tokens, "tile", axis=1, tiled=True),
        lax.all_gather(slot_hidden, "tile", axis=1, tiled=True),
    )
    column_tokens, column_hidden = (
        lax.all_to_all(full_tokens, "dp", split_axis=1, concat_axis=0, tiled=True),
        lax.all_to_all(full_hidden, "dp", split_axis=1, concat_axis=0, tiled=True),
    )
    pieces = side_by_side((slot_tokens, slot_hidden), "dp", 0, 1)
    gram_tokens = contract(pieces[0], column_tokens)
    gram_hidden = contract(pieces[1], column_hidden)
    return ((gram_tokens * factor)[None], (gram_hidden * factor)[None])


def solution(mesh):
    placed = (
        P(("dp", "expert"), "tile"),
        P(("dp", "expert"), None, "tile"),
        P(("dp", "expert"), None),
        P(("dp", "expert")),
    )
    return jax.shard_map(
        on_device,
        mesh=mesh,
        in_specs=placed,
        out_specs=(P("expert", "tile", "dp"), P("expert", "tile", "dp")),
        check_vma=False,
    )
```

profile of v0, /device:TPU:1, one launch (start us, length us, event | category | flops | bytes accessed | tf_op | source)
XLA Modules:
  0.0 226.2 jit_solution(10405702550066354825)
XLA Ops:
  7.9 0.8 copy.33
  8.7 0.1 eq.43
  8.8 0.1 fusion.11
  8.9 0.2 reduce_window_sum.11
  9.1 0.2 fusion.12
  9.3 0.1 rem.32
  9.5 0.1 div.25
  9.8 0.2 ne.82
  10.1 1.2 reshape.98
  11.2 0.7 fusion.18
  11.9 0.1 convert_reduce_fusion
  12.1 0.3 convolution_convert_fusion.1
  12.3 0.3 convolution_convert_fusion
  12.8 0.5 all_to_all.40
  13.3 49.6 %all_to_all.56 = bf16[64,3,2816]{2,1,0:T(4,128)(2,1)S(1)} all-to-all(bf16[64,3,2816]{2,1,0:T(4,128)(2,1)S(1)} %all_to_all.40), channel_id=1, replica_groups=mesh['dp'=8,'expert'=8,'tile'=4] {'dp','expert'}, dimensions={0} | all-to-all | bytes 2162688 | tf_op jit(solution)/shard_map/all_to_all | solution.py:10
  62.8 0.9 all_to_all.42
  63.8 1.0 split.19
  64.8 0.8 split.17
  65.7 0.7 all-gather.4.cloned.1.call-update
  66.4 0.6 broadcast_in_dim.18
  67.0 6.7 %all-to-all-start.2 = ((f32[64,1,8]{2,1,0:T(1,128)}), f32[64,1,8]{2,1,0:T(1,128)S(1)}, u32[]{:S(2)}, u32[]{:S(2)}) async-start(f32[64,1,8]{2,1,0:T(1,128)} %broadcast_in_dim.18), calls=%async_computation.2 | async-start | bytes 65536 | tf_op jit(solution)/shard_map/all_to_all | solution.py:16
  73.8 27.1 %all-gather.8.cloned.1.call-done = bf16[192,7168]{1,0:T(8,128)(2,1)} async-done(((bf16[192,1792]{1,0:T(8,128)(2,1)}), bf16[192,7168]{1,0:T(8,128)(2,1)}) %all-gather.8.cloned.1.call-update) | async-done | bytes 2752528 | tf_op jit(solution)/shard_map/all_gather | solution.py:88
  100.9 3.7 %copy.49 = bf16[24,8,8,896]{3,2,0,1:T(8,128)(2,1)} copy(bf16[24,8,8,896]{3,2,1,0:T(8,128)(2,1)} %bitcast.27) | data formatting | bytes 5505024 | tf_op jit(solution)/shard_map/all_to_all | solution.py:92
  104.6 5.1 %all-to-all-start.3 = ((bf16[192,8,896]{2,0,1:T(8,128)(2,1)}), bf16[192,8,896]{2,0,1:T(8,128)(2,1)S(1)}, u32[]{:S(2)}, u32[]{:S(2)}) async-start(bf16[192,8,896]{2,0,1:T(8,128)(2,1)} %bitcast.22), calls=%async_computation.3 | async-start | bytes 5505024 | tf_op jit(solution)/shard_map/all_to_all | solution.py:92
  109.7 22.2 %all-gather.6.cloned.1.call-done = bf16[192,4096]{1,0:T(8,128)(2,1)} async-done(((bf16[192,1024]{1,0:T(8,128)(2,1)}), bf16[192,4096]{1,0:T(8,128)(2,1)}) %all-gather.6.cloned.1.call-update) | async-done | bytes 1572880 | tf_op jit(solution)/shard_map/all_gather | solution.py:87
  131.9 2.7 %copy.50 = bf16[24,8,8,512]{3,2,0,1:T(8,128)(2,1)} copy(bf16[24,8,8,512]{3,2,1,0:T(8,128)(2,1)} %bitcast.28) | data formatting | bytes 3145728 | tf_op jit(solution)/shard_map/all_to_all | solution.py:91
  134.6 8.4 %all-to-all-done.3 = bf16[192,8,896]{2,0,1:T(8,128)(2,1)S(1)} async-done(((bf16[192,8,896]{2,0,1:T(8,128)(2,1)}), bf16[192,8,896]{2,0,1:T(8,128)(2,1)S(1)}, u32[]{:S(2)}, u32[]{:S(2)}) %all-to-all-start.3) | async-done | bytes 2752544 | tf_op jit(solution)/shard_map/all_to_all | solution.py:92
  142.9 5.2 %all-to-all-start.1 = ((bf16[192,8,512]{2,0,1:T(8,128)(2,1)}), bf16[192,8,512]{2,0,1:T(8,128)(2,1)}, u32[]{:S(2)}, u32[]{:S(2)}) async-start(bf16[192,8,512]{2,0,1:T(8,128)(2,1)} %bitcast.23), calls=%async_computation.1 | async-start | bytes 3145728 | tf_op jit(solution)/shard_map/all_to_all | solution.py:91
  148.2 0.6 fusion.22
  149.5 55.0 %all-gather.4.cloned.1.call-done = bf16[1536,2816]{1,0:T(8,128)(2,1)} async-done(((bf16[192,2816]{1,0:T(8,128)(2,1)}), bf16[1536,2816]{1,0:T(8,128)(2,1)}) %all-gather.4.cloned.1.call-update) | async-done | bytes 8650768 | tf_op jit(solution)/shard_map/all_gather | solution.py:30
  204.5 9.6 %multiply_bitcast_fusion = f32[1,1792,896]{2,1,0:T(8,128)} fusion(bf16[1536,896]{1,0:T(8,128)(2,1)S(1)} %bitcast.26, bf16[1536,2816]{1,0:T(8,128)(2,1)} %all-gather.4.cloned.1.call-done, f32[]{:T(128)S(6)} %div.27), kind=kOutput, calls=%fused_computation | convolution fusion | flops 4934107136 | bytes 14680068 | tf_op jit(solution)/shard_map/dot_general | solution.py:34
  214.2 5.5 %multiply_bitcast_fusion.1 = f32[1,1024,512]{2,1,0:T(8,128)} fusion(bf16[1536,512]{1,0:T(8,128)(2,1)} %bitcast.2, bf16[1536,2816]{1,0:T(8,128)(2,1)} %all-gather.4.cloned.1.call-done, f32[]{:T(128)S(6)} %div.27), kind=kOutput, calls=%fused_computation.7 | convolution fusion | flops 1611137024 | bytes 6815748 | tf_op jit(solution)/shard_map/dot_general | solution.py:34
  (20 shorter events, 0.6 us)
Async XLA Ops:
  7.2 4.9 %copy-start = (bf16[64,1024]{1,0:T(8,128)(2,1)S(1)}, bf16[64,1024]{1,0:T(8,128)(2,1)}, u32[]{:S(2)}) copy-start(bf16[64,1024]{1,0:T(8,128)(2,1)} %param.4) | copy-start | bytes 393220
  7.2 93.7 %all-gather.8.cloned.1.call-start = ((), (), s32[]{:S(2)}) async-start(), calls=%async_computation.6 | async-start | bytes 3440640 | tf_op jit(solution)/shard_map/all_gather | solution.py:88
  63.8 2.0 copy-start.1
  64.8 67.1 %all-gather.6.cloned.1.call-start = ((), (), s32[]{:S(2)}) async-start(), calls=%async_computation.5 | async-start | bytes 1966080 | tf_op jit(solution)/shard_map/all_gather | solution.py:87
  65.7 138.8 %all-gather.4.cloned.1.call-start = ((), (), s32[]{:S(2)}) async-start(), calls=%async_computation.4 | async-start | bytes 9732096 | tf_op jit(solution)/shard_map/all_gather | solution.py:30
  67.0 37.5 %all-to-all-start.2 = ((f32[64,1,8]{2,1,0:T(1,128)}), f32[64,1,8]{2,1,0:T(1,128)S(1)}, u32[]{:S(2)}, u32[]{:S(2)}) async-start(f32[64,1,8]{2,1,0:T(1,128)} %broadcast_in_dim.18), calls=%async_computation.2 | async-start | bytes 65536 | tf_op jit(solution)/shard_map/all_to_all | solution.py:16
  104.6 38.4 %all-to-all-start.3 = ((bf16[192,8,896]{2,0,1:T(8,128)(2,1)}), bf16[192,8,896]{2,0,1:T(8,128)(2,1)S(1)}, u32[]{:S(2)}, u32[]{:S(2)}) async-start(bf16[192,8,896]{2,0,1:T(8,128)(2,1)} %bitcast.22), calls=%async_computation.3 | async-start | bytes 5505024 | tf_op jit(solution)/shard_map/all_to_all | solution.py:92
  142.9 71.2 %all-to-all-start.1 = ((bf16[192,8,512]{2,0,1:T(8,128)(2,1)}), bf16[192,8,512]{2,0,1:T(8,128)(2,1)}, u32[]{:S(2)}, u32[]{:S(2)}) async-start(bf16[192,8,512]{2,0,1:T(8,128)(2,1)} %bitcast.23), calls=%async_computation.1 | async-start | bytes 3145728 | tf_op jit(solution)/shard_map/all_to_all | solution.py:91
Sparse Core Ops, SparseCore 0:
  64.9 35.9 all-gather.7
  102.7 29.1 all-gather.5
  133.7 70.7 all-gather.3
where the time goes:
time: 227 us; the launch traced here: 226 us
  waiting for transfers between devices  113 us (50%)
  blocking collectives  49.6 us (22%)
  starting transfers between devices  17.1 us (8%)
  matrix products  15.8 us (7%)
  between operations  15.3 us (7%)
  local copies, waits for them, and re-layouts  13 us (6%)
    all_gather x1, waiting for transfers between devices, side_by_side(): lax.all_gather(both, axis, axis=dim, tiled=True)  55 us
    all_to_all x1, blocking collectives, sent_together(): lax.all_to_all(both, axis, split_axis=split_dim, concat_axis=concat_dim,...  49.6 us
    all_gather x1, waiting for transfers between devices, on_device(): lax.all_gather(slot_hidden, 'tile', axis=1, tiled=True)  27.1 us
    all_gather x1, waiting for transfers between devices, on_device(): lax.all_gather(slot_tokens, 'tile', axis=1, tiled=True)  22.2 us
    dot_general x2, matrix products, contract(): lax.dot_general(left, right, (((0,), (0,)), ((), ())), preferred_element_...  15.2 us
    all_to_all x1, waiting for transfers between devices, on_device(): lax.all_to_all(full_hidden, 'dp', split_axis=1, concat_axis=0, tiled=True)  8.35 us
    all_to_all x1, starting transfers between devices, from_everyone(): return lax.all_to_all(copies, axis, split_axis=0, concat_axis=0, tiled=True)  6.72 us
    all_to_all x1, starting transfers between devices, on_device(): lax.all_to_all(full_tokens, 'dp', split_axis=1, concat_axis=0, tiled=True)  5.17 us
  transfers between devices with their start and end apart: 6, of which 4 were waited for; matrix products, arithmetic and copies ran while one was open for 8% of the time, Pallas kernels for 0%

commit v1 on v0

--- a/solution.py
+++ b/solution.py
@@ -84,7 +84,7 @@
     )
     factor = 2.0 / jnp.maximum(own_count, 1.0)
     full_tokens, full_hidden = (
-        lax.all_gather(slot_tokens, "tile", axis=1, tiled=True),
+        jnp.concatenate(lax.all_gather(slot_tokens, "tile"), axis=1),
         lax.all_gather(slot_hidden, "tile", axis=1, tiled=True),
     )
     column_tokens, column_hidden = (

time: 227 us -> 227 us (level)
    all_gather x0 -> x1, local copies, waits for them, and re-layouts: none -> 2.62 us  [on_device(): lax.all_gather(slot_tokens, 'tile')]
  transfers between devices with their start and end apart: 6 -> 6, of which waited for: 4 -> 4; matrix products, arithmetic and copies ran while one was open for 8% -> 9% of each run, Pallas kernels for 0% -> 0%
where the time goes in v1:
time: 227 us
  waiting for transfers between devices  112 us (49%)
  blocking collectives  49.6 us (22%)
  starting transfers between devices  16.5 us (7%)
  matrix products  16.1 us (7%)
  between operations  15.3 us (7%)
  local copies, waits for them, and re-layouts  15 us (7%)
    all_gather x1, waiting for transfers between devices, side_by_side(): lax.all_gather(both, axis, axis=dim, tiled=True)  55.6 us
    all_to_all x1, blocking collectives, sent_together(): lax.all_to_all(both, axis, split_axis=split_dim, concat_axis=concat_dim,...  49.6 us
    all_gather x1, waiting for transfers between devices, on_device(): lax.all_gather(slot_hidden, 'tile', axis=1, tiled=True)  27.1 us
    all_gather x1, waiting for transfers between devices, on_device(): lax.all_gather(slot_tokens, 'tile')  22.1 us
    dot_general x2, matrix products, contract(): lax.dot_general(left, right, (((0,), (0,)), ((), ())), preferred_element_...  15.5 us
    all_to_all x1, starting transfers between devices, from_everyone(): return lax.all_to_all(copies, axis, split_axis=0, concat_axis=0, tiled=True)  6.72 us
    all_to_all x1, waiting for transfers between devices, on_device(): lax.all_to_all(full_hidden, 'dp', split_axis=1, concat_axis=0, tiled=True)  6.5 us
    all_to_all x1, starting transfers between devices, on_device(): lax.all_to_all(full_hidden, 'dp', split_axis=1, concat_axis=0, tiled=True)  5.15 us
  transfers between devices with their start and end apart: 6, of which 4 were waited for; matrix products, arithmetic and copies ran while one was open for 9% of the time, Pallas kernels for 0%

profile of v1, /device:TPU:1, one launch (start us, length us, event | category | flops | bytes accessed | tf_op | source)
XLA Modules:
  0.0 226.5 jit_solution(17701793265951929657)
XLA Ops:
  7.9 0.8 copy.43
  8.7 0.1 eq.43
  8.9 0.2 reduce_window_sum.11
  9.1 0.2 fusion.12
  9.3 0.1 rem.32
  9.5 0.1 div.25
  9.8 0.2 ne.82
  10.1 1.2 reshape.103
  11.2 0.7 fusion.18
  12.1 0.3 convolution_convert_fusion.1
  12.3 0.3 convolution_convert_fusion
  12.8 0.5 all_to_all.40
  13.3 49.6 %all_to_all.56 = bf16[64,3,2816]{2,1,0:T(4,128)(2,1)S(1)} all-to-all(bf16[64,3,2816]{2,1,0:T(4,128)(2,1)S(1)} %all_to_all.40), channel_id=1, replica_groups=mesh['dp'=8,'expert'=8,'tile'=4] {'dp','expert'}, dimensions={0} | all-to-all | bytes 2162688 | tf_op jit(solution)/shard_map/all_to_all | solution.py:10
  62.8 0.9 all_to_all.42
  63.8 1.0 split.19
  64.8 0.8 split.17
  65.7 0.7 all-gather.5.cloned.1.call-update
  66.4 0.6 broadcast_in_dim.18
  67.0 6.7 %all-to-all-start.2 = ((f32[64,1,8]{2,1,0:T(1,128)}), f32[64,1,8]{2,1,0:T(1,128)S(1)}, u32[]{:S(2)}, u32[]{:S(2)}) async-start(f32[64,1,8]{2,1,0:T(1,128)} %broadcast_in_dim.18), calls=%async_computation.2 | async-start | bytes 65536 | tf_op jit(solution)/shard_map/all_to_all | solution.py:16
  73.8 27.1 %all-gather.7.cloned.1.call-done = bf16[192,7168]{1,0:T(8,128)(2,1)} async-done(((bf16[192,1792]{1,0:T(8,128)(2,1)}), bf16[192,7168]{1,0:T(8,128)(2,1)}) %all-gather.7.cloned.1.call-update) | async-done | bytes 2752528 | tf_op jit(solution)/shard_map/all_gather | solution.py:88
  100.9 3.7 %copy.59 = bf16[24,8,8,896]{3,2,0,1:T(8,128)(2,1)} copy(bf16[24,8,8,896]{3,2,1,0:T(8,128)(2,1)} %bitcast.27) | data formatting | bytes 5505024 | tf_op jit(solution)/shard_map/all_to_all | solution.py:92
  104.6 5.1 %all-to-all-start.3 = ((bf16[192,8,896]{2,0,1:T(8,128)(2,1)}), bf16[192,8,896]{2,0,1:T(8,128)(2,1)}, u32[]{:S(2)}, u32[]{:S(2)}) async-start(bf16[192,8,896]{2,0,1:T(8,128)(2,1)} %bitcast.22), calls=%async_computation.3 | async-start | bytes 5505024 | tf_op jit(solution)/shard_map/all_to_all | solution.py:92
  109.7 22.1 %all-gather.9.cloned.1.call-done = bf16[768,1024]{1,0:T(8,128)(2,1)} async-done(((bf16[192,1024]{1,0:T(8,128)(2,1)}), bf16[768,1024]{1,0:T(8,128)(2,1)}) %all-gather.9.cloned.1.call-update) | async-done | bytes 1572880 | tf_op jit(solution)/shard_map/all_gather | solution.py:87
  131.9 2.6 %copy.60 = bf16[4,192,1024]{2,0,1:T(4,128)(2,1)S(1)} copy(bf16[4,192,1024]{2,1,0:T(8,128)(2,1)} %bitcast.28) | data formatting | bytes 3145728 | tf_op jit(solution)/shard_map/all_gather | solution.py:87
  134.5 0.4 all_to_all.43
  134.9 1.6 copy.52
  136.6 6.5 %all-to-all-done.3 = bf16[192,8,896]{2,0,1:T(8,128)(2,1)} async-done(((bf16[192,8,896]{2,0,1:T(8,128)(2,1)}), bf16[192,8,896]{2,0,1:T(8,128)(2,1)}, u32[]{:S(2)}, u32[]{:S(2)}) %all-to-all-start.3) | async-done | bytes 2752544 | tf_op jit(solution)/shard_map/all_to_all | solution.py:92
  143.1 4.5 %all-to-all-start.1 = ((bf16[192,8,512]{2,0,1:T(8,128)(2,1)}), bf16[192,8,512]{2,0,1:T(8,128)(2,1)S(1)}, u32[]{:S(2)}, u32[]{:S(2)}) async-start(bf16[192,8,512]{2,0,1:T(8,128)(2,1)} %copy.52), calls=%async_computation.1 | async-start | bytes 3145728 | tf_op jit(solution)/shard_map/all_to_all | solution.py:91
  147.7 0.6 fusion.22
  149.0 55.6 %all-gather.5.cloned.1.call-done = bf16[1536,2816]{1,0:T(8,128)(2,1)} async-done(((bf16[192,2816]{1,0:T(8,128)(2,1)}), bf16[1536,2816]{1,0:T(8,128)(2,1)}) %all-gather.5.cloned.1.call-update) | async-done | bytes 8650768 | tf_op jit(solution)/shard_map/all_gather | solution.py:30
  204.5 10.4 %multiply_bitcast_fusion = f32[1,1792,896]{2,1,0:T(8,128)} fusion(bf16[1536,896]{1,0:T(8,128)(2,1)} %bitcast.7, bf16[1536,2816]{1,0:T(8,128)(2,1)} %all-gather.5.cloned.1.call-done, f32[]{:T(128)S(6)} %div.27), kind=kOutput, calls=%fused_computation | convolution fusion | flops 4934107136 | bytes 14680068 | tf_op jit(solution)/shard_map/dot_general | solution.py:34
  215.0 5.1 %multiply_bitcast_fusion.1 = f32[1,1024,512]{2,1,0:T(8,128)} fusion(bf16[1536,512]{1,0:T(8,128)(2,1)S(1)} %bitcast.29, bf16[1536,2816]{1,0:T(8,128)(2,1)} %all-gather.5.cloned.1.call-done, f32[]{:T(128)S(6)} %div.27), kind=kOutput, calls=%fused_computation.7 | convolution fusion | flops 1611137024 | bytes 6815748 | tf_op jit(solution)/shard_map/dot_general | solution.py:34
  (22 shorter events, 0.8 us)
Async XLA Ops:
  7.2 4.9 %copy-start = (bf16[64,1024]{1,0:T(8,128)(2,1)S(1)}, bf16[64,1024]{1,0:T(8,128)(2,1)}, u32[]{:S(2)}) copy-start(bf16[64,1024]{1,0:T(8,128)(2,1)} %param.4) | copy-start | bytes 393220
  7.2 93.7 %all-gather.7.cloned.1.call-start = ((), (), s32[]{:S(2)}) async-start(), calls=%async_computation.5 | async-start | bytes 3440640 | tf_op jit(solution)/shard_map/all_gather | solution.py:88
  63.8 2.0 copy-start.1
  64.8 67.1 %all-gather.9.cloned.1.call-start = ((), (), s32[]{:S(2)}) async-start(), calls=%async_computation.6 | async-start | bytes 1966080 | tf_op jit(solution)/shard_map/all_gather | solution.py:87
  65.7 138.8 %all-gather.5.cloned.1.call-start = ((), (), s32[]{:S(2)}) async-start(), calls=%async_computation.4 | async-start | bytes 9732096 | tf_op jit(solution)/shard_map/all_gather | solution.py:30
  67.0 37.5 %all-to-all-start.2 = ((f32[64,1,8]{2,1,0:T(1,128)}), f32[64,1,8]{2,1,0:T(1,128)S(1)}, u32[]{:S(2)}, u32[]{:S(2)}) async-start(f32[64,1,8]{2,1,0:T(1,128)} %broadcast_in_dim.18), calls=%async_computation.2 | async-start | bytes 65536 | tf_op jit(solution)/shard_map/all_to_all | solution.py:16
  104.6 38.5 %all-to-all-start.3 = ((bf16[192,8,896]{2,0,1:T(8,128)(2,1)}), bf16[192,8,896]{2,0,1:T(8,128)(2,1)}, u32[]{:S(2)}, u32[]{:S(2)}) async-start(bf16[192,8,896]{2,0,1:T(8,128)(2,1)} %bitcast.22), calls=%async_computation.3 | async-start | bytes 5505024 | tf_op jit(solution)/shard_map/all_to_all | solution.py:92
  143.1 71.9 %all-to-all-start.1 = ((bf16[192,8,512]{2,0,1:T(8,128)(2,1)}), bf16[192,8,512]{2,0,1:T(8,128)(2,1)S(1)}, u32[]{:S(2)}, u32[]{:S(2)}) async-start(bf16[192,8,512]{2,0,1:T(8,128)(2,1)} %copy.52), calls=%async_computation.1 | async-start | bytes 3145728 | tf_op jit(solution)/shard_map/all_to_all | solution.py:91
Sparse Core Ops, SparseCore 0:
  64.9 35.9 all-gather.6
  102.7 29.1 all-gather.8
  133.7 70.7 all-gather.4
